TPU v7x, 32 devices: a whole 2x2x4 slice. The times are simulated.
32 devices in a mesh: row: 4 (over y, x), rhs: 8 (over z, core).
Axes of the slice: x: 2, y: 2, z: 4, core: 2. Of those that a mesh axis runs over, the one named last changes fastest.
Arguments:
- factor: float32 [3072, 12, 256], P('row', None, 'rhs'), as said below
- inverses: float32 [12, 256, 256], P('row'), as said below
- right_side: float32 [3072, 4096], P('row', 'rhs'), may hold values from -6 to 6
Outputs:
- solution: float32 [3072, 4096], P('row', 'rhs')
Inputs may be any that keep to these rules, and one draw needn't show every extreme that they name: factor[i, j, c] is zero unless j is less than i // 256. Each inverses[p] is lower triangular with a positive diagonal.
All inputs are finite; a program needn't handle non-finite values.
Results may differ from a plain program's by a relative error of at most 0.0001.
Values sent between devices are 32-bit elements; how exact they have to be, the bound alone decides.
No kernel may reach another device: no remote copies, remote signals or barrier semaphores. Data moves between devices by JAX's collectives and lax.ppermute only.
A program may use at most 128 MiB of HBM per device.

v0:
```python
import jax
import jax.numpy as jnp
from jax import lax
from jax.sharding import PartitionSpec as P


def from_root(block, axis, owner):
    block = jnp.where(lax.axis_index(axis) == owner, block, jnp.zeros_like(block))
    return lax.psum(block, axis)


def mult(left, right):
    return jnp.dot(left, right, preferred_element_type=jnp.float32, precision=lax.Precision.HIGHEST)


def body(factor, inverses, right_side):
    block = right_side.shape[0]
    panel = inverses.shape[1]
    per_block = inverses.shape[0]
    rounds = lax.axis_size("row")
    mine = lax.axis_index("row")
    gathered = lax.all_gather(factor, "rhs", axis=2, tiled=True)

    def fetch(first, count):
        return lax.dynamic_slice_in_dim(gathered, first, count, 1)

    def apply_tiles(residual, tiles, solved):
        return residual - mult(tiles.reshape(block, -1), solved)

    solution = jnp.zeros_like(right_side)

    def step_block(index, state):
        residual, solution = state
        tiles = fetch(index * per_block, per_block)
        working = residual
        pieces = []
        for inner in range(per_block):
            solved_part = mult(inverses[inner], working[inner * panel : (inner + 1) * panel])
            pieces.append(solved_part)
            working = working - mult(tiles[:, inner, :], solved_part)
        solved = from_root(jnp.concatenate(pieces, axis=0), "row", index)
        residual = apply_tiles(residual, tiles, solved)
        solution = jnp.where(mine == index, solved, solution)
        return (residual, solution)

    residual, solution = lax.fori_loop(0, rounds, step_block, (right_side, solution))
    return solution


def solution(mesh):
    placed = (P("row", None, "rhs"), P("row", None, None), P("row", "rhs"))
    return jax.shard_map(
        body, mesh=mesh, in_specs=placed, out_specs=P("row", "rhs"), check_vma=False
    )
```

profile of v0, /device:TPU:0, one launch (start us, length us, event | category | flops | bytes accessed | tf_op | source)
XLA Modules:
  0.0 417.8 jit_solution(4897587918877244173)
XLA Ops:
  6.5 0.7 all-gather.2.cloned.1.call-update
  7.3 95.1 %all-gather.2.cloned.1.call-done = f32[768,12,256]{0,2,1:T(8,128)} async-done(((f32[768,12,32]{0,2,1:T(8,128)}), f32[768,12,256]{0,2,1:T(8,128)}) %all-gather.2.cloned.1.call-update) | async-done | bytes 9437200 | tf_op jit(solution)/shard_map/all_gather | solution.py:22
  102.4 307.8 %while.16 = (s32[]{:T(128)}, f32[768,512]{1,0:T(8,128)S(1)}, f32[768,512]{1,0:T(8,128)S(1)}, f32[768,12,256]{0,2,1:T(8,128)}, f32[3,256,256]{2,1,0:T(8,128)}, /*...) while((s32[]{:T(128)}, f32[768,512]{1,0:T(8,128)S(1)}, ...), condition=%wide.region_2.3_spmd.clone, body=%wide.region_0.2_spmd.clone.sunk | while | flops 7251034112 | bytes 50332000 | solution.py:46
  102.4 1.6 fusion.39
  104.0 2.7 convolution_subtract_fusion.4
  106.7 0.6 fusion.40
  107.3 2.6 fusion.41
  109.9 0.7 convolution_bitcast_fusion.2
  110.6 1.3 maximum_select_fusion.2
  111.9 3.2 constant_dynamic-slice_fusion.2
  115.1 56.1 %all-reduce.2.cloned.1.call-done = f32[768,512]{1,0:T(8,128)} async-done(((f32[768,512]{1,0:T(8,128)}), f32[768,512]{1,0:T(8,128)}) %all-reduce.2.cloned.1.call-update) | async-done | bytes 1572880 | tf_op jit(solution)/shard_map/while/body/eval_jaxpr/psum | solution.py:9
  171.2 6.4 %convolution_subtract_fusion.5 = f32[768,512]{1,0:T(8,128)S(1)} fusion(f32[768,512]{1,0:T(8,128)S(1)} %get-tuple-element.198, f32[768,768]{0,1:T(8,128)} %bitcast.47, f32[768,512]{1,0:T(8,128)} %all-reduce.2.cloned.1.call-done), kind=kOutput, calls=%fused_computation.3.clone.1 | convolution fusion | flops 3624271872 | bytes 7077888 | tf_op jit(solution)/shard_map/while/body/eval_jaxpr/dot_general | solution.py:13
  177.6 0.5 select_select_fusion.2
  178.1 0.0 all-reduce.2.cloned.1.call-start
  178.2 1.6 fusion.39
  179.8 2.7 convolution_subtract_fusion.4
  182.4 0.6 fusion.40
  183.1 2.6 fusion.41
  185.7 0.7 convolution_bitcast_fusion.2
  186.3 1.3 maximum_select_fusion.2
  187.6 0.0 all-reduce.2.cloned.1.call-update
  187.7 3.2 constant_dynamic-slice_fusion.2
  190.9 57.7 %all-reduce.2.cloned.1.call-done = f32[768,512]{1,0:T(8,128)} async-done(((f32[768,512]{1,0:T(8,128)}), f32[768,512]{1,0:T(8,128)}) %all-reduce.2.cloned.1.call-update) | async-done | bytes 1572880 | tf_op jit(solution)/shard_map/while/body/eval_jaxpr/psum | solution.py:9
  248.5 6.4 %convolution_subtract_fusion.5 = f32[768,512]{1,0:T(8,128)S(1)} fusion(f32[768,512]{1,0:T(8,128)S(1)} %get-tuple-element.198, f32[768,768]{0,1:T(8,128)} %bitcast.47, f32[768,512]{1,0:T(8,128)} %all-reduce.2.cloned.1.call-done), kind=kOutput, calls=%fused_computation.3.clone.1 | convolution fusion | flops 3624271872 | bytes 7077888 | tf_op jit(solution)/shard_map/while/body/eval_jaxpr/dot_general | solution.py:13
  255.0 0.5 select_select_fusion.2
  255.5 0.0 all-reduce.2.cloned.1.call-start
  255.5 1.6 fusion.39
  257.1 2.7 convolution_subtract_fusion.4
  259.8 0.6 fusion.40
  260.4 2.6 fusion.41
  263.0 0.7 convolution_bitcast_fusion.2
  263.7 1.3 maximum_select_fusion.2
  265.0 3.2 constant_dynamic-slice_fusion.2
  268.2 57.7 %all-reduce.2.cloned.1.call-done = f32[768,512]{1,0:T(8,128)} async-done(((f32[768,512]{1,0:T(8,128)}), f32[768,512]{1,0:T(8,128)}) %all-reduce.2.cloned.1.call-update) | async-done | bytes 1572880 | tf_op jit(solution)/shard_map/while/body/eval_jaxpr/psum | solution.py:9
  325.9 6.4 %convolution_subtract_fusion.5 = f32[768,512]{1,0:T(8,128)S(1)} fusion(f32[768,512]{1,0:T(8,128)S(1)} %get-tuple-element.198, f32[768,768]{0,1:T(8,128)} %bitcast.47, f32[768,512]{1,0:T(8,128)} %all-reduce.2.cloned.1.call-done), kind=kOutput, calls=%fused_computation.3.clone.1 | convolution fusion | flops 3624271872 | bytes 7077888 | tf_op jit(solution)/shard_map/while/body/eval_jaxpr/dot_general | solution.py:13
  332.3 0.5 select_select_fusion.2
  332.8 0.0 all-reduce.2.cloned.1.call-start
  332.9 1.6 fusion.39
  334.5 2.7 convolution_subtract_fusion.4
  337.1 0.6 fusion.40
  337.8 2.6 fusion.41
  340.4 0.7 convolution_bitcast_fusion.2
  341.0 1.3 maximum_select_fusion.2
  342.4 3.2 constant_dynamic-slice_fusion.2
  345.6 57.7 %all-reduce.2.cloned.1.call-done = f32[768,512]{1,0:T(8,128)} async-done(((f32[768,512]{1,0:T(8,128)}), f32[768,512]{1,0:T(8,128)}) %all-reduce.2.cloned.1.call-update) | async-done | bytes 1572880 | tf_op jit(solution)/shard_map/while/body/eval_jaxpr/psum | solution.py:9
  403.3 6.4 %convolution_subtract_fusion.5 = f32[768,512]{1,0:T(8,128)S(1)} fusion(f32[768,512]{1,0:T(8,128)S(1)} %get-tuple-element.198, f32[768,768]{0,1:T(8,128)} %bitcast.47, f32[768,512]{1,0:T(8,128)} %all-reduce.2.cloned.1.call-done), kind=kOutput, calls=%fused_computation.3.clone.1 | convolution fusion | flops 3624271872 | bytes 7077888 | tf_op jit(solution)/shard_map/while/body/eval_jaxpr/dot_general | solution.py:13
  409.7 0.5 select_select_fusion.2
  410.2 1.1 copy-done.2
  (25 shorter events, 0.1 us)
Async XLA Ops:
  6.5 95.9 %copy-start = (f32[768,512]{1,0:T(8,128)S(1)}, f32[768,512]{1,0:T(8,128)}, u32[]{:S(2)}) copy-start(f32[768,512]{1,0:T(8,128)} %param.7) | copy-start | bytes 4718596
  6.5 95.9 %all-gather.2.cloned.1.call-start = ((), (), s32[]{:S(2)}) async-start(), calls=%async_computation | async-start | bytes 10616832 | tf_op jit(solution)/shard_map/all_gather | solution.py:22
  102.4 68.8 %all-reduce.2.cloned.1.call-start = ((), (), s32[]{:S(2)}) async-start(), calls=%async_computation.1 | async-start | bytes 3145728 | tf_op jit(solution)/shard_map/while/body/eval_jaxpr/psum | solution.py:9
  104.0 2.7 copy-start.3
  171.2 6.4 %copy-start.1 = (f32[768,512]{1,0:T(8,128)S(1)}, f32[768,512]{1,0:T(8,128)}, u32[]{:S(2)}) copy-start(f32[768,512]{1,0:T(8,128)} %all-reduce.2.cloned.1.call-done) | copy-start | bytes 4718596 | tf_op jit(solution)/shard_map/while
  178.1 70.4 %all-reduce.2.cloned.1.call-start = ((), (), s32[]{:S(2)}) async-start(), calls=%async_computation.1 | async-start | bytes 3145728 | tf_op jit(solution)/shard_map/while/body/eval_jaxpr/psum | solution.py:9
  179.7 2.7 copy-start.3
  248.5 6.4 %copy-start.1 = (f32[768,512]{1,0:T(8,128)S(1)}, f32[768,512]{1,0:T(8,128)}, u32[]{:S(2)}) copy-start(f32[768,512]{1,0:T(8,128)} %all-reduce.2.cloned.1.call-done) | copy-start | bytes 4718596 | tf_op jit(solution)/shard_map/while
  255.5 70.4 %all-reduce.2.cloned.1.call-start = ((), (), s32[]{:S(2)}) async-start(), calls=%async_computation.1 | async-start | bytes 3145728 | tf_op jit(solution)/shard_map/while/body/eval_jaxpr/psum | solution.py:9
  257.1 2.7 copy-start.3
  325.9 6.4 %copy-start.1 = (f32[768,512]{1,0:T(8,128)S(1)}, f32[768,512]{1,0:T(8,128)}, u32[]{:S(2)}) copy-start(f32[768,512]{1,0:T(8,128)} %all-reduce.2.cloned.1.call-done) | copy-start | bytes 4718596 | tf_op jit(solution)/shard_map/while
  332.8 70.4 %all-reduce.2.cloned.1.call-start = ((), (), s32[]{:S(2)}) async-start(), calls=%async_computation.1 | async-start | bytes 3145728 | tf_op jit(solution)/shard_map/while/body/eval_jaxpr/psum | solution.py:9
  334.5 2.7 copy-start.3
  403.3 6.4 %copy-start.1 = (f32[768,512]{1,0:T(8,128)S(1)}, f32[768,512]{1,0:T(8,128)}, u32[]{:S(2)}) copy-start(f32[768,512]{1,0:T(8,128)} %all-reduce.2.cloned.1.call-done) | copy-start | bytes 4718596 | tf_op jit(solution)/shard_map/while
  410.2 1.1 copy-start.2
Sparse Core Ops, SparseCore 0:
  8.9 93.4 all-gather.1
  112.0 59.1 all-reduce.1
  187.8 60.7 all-reduce.1
  265.1 60.7 all-reduce.1
  342.5 60.7 all-reduce.1
where the time goes:
time: 418 us
  waiting for transfers between devices  325 us (78%)
  matrix products  58 us (14%)
  local copies, waits for them, and re-layouts  14 us (3%)
  between operations  13.1 us (3%)
  other arithmetic  7.15 us (2%)
    psum x4, waiting for transfers between devices, from_root(): return lax.psum(block, axis)  229 us
    all_gather x1, waiting for transfers between devices, body(): gathered = lax.all_gather(factor, 'rhs', axis=2, tiled=True)  95.1 us
    dot_general x24, matrix products, mult(): jnp.dot(left, right, preferred_element_type=jnp.float32, precision=lax.Pr...  58 us
    dynamic_slice x4, local copies, waits for them, and re-layouts, fetch(): return lax.dynamic_slice_in_dim(gathered, first, count, 1)  12.8 us
  transfers between devices with their start and end apart: 5, of which 5 were waited for; matrix products, arithmetic and copies ran while one was open for 3% of the time, Pallas kernels for 0%

commit v1 on v0

--- a/solution.py
+++ b/solution.py
@@ -6,7 +6,7 @@
 
 def from_root(block, axis, owner):
     block = jnp.where(lax.axis_index(axis) == owner, block, jnp.zeros_like(block))
-    return lax.psum(block, axis)
+    return jnp.sum(lax.all_gather(block, axis), axis=0)
 
 
 def mult(left, right):

time: 418 us -> 485 us (1.16)
  waiting for transfers between devices: 325 us -> 362 us
  other arithmetic: 7.15 us -> 22 us
  local copies, waits for them, and re-layouts: 14 us -> 22.1 us
  matrix products: 58 us -> 64 us
    all_gather x0 -> x4, waiting for transfers between devices: none -> 266 us  [from_root(): return jnp.sum(lax.all_gather(block, axis), axis=0)]
    psum x4 -> x0, waiting for transfers between devices: 229 us -> none  [from_root(): return lax.psum(block, axis)]
    reduce_sum x0 -> x4, other arithmetic: none -> 14.8 us  [from_root(): return jnp.sum(lax.all_gather(block, axis), axis=0)]
    while x16 -> x24, local copies, waits for them, and re-layouts: 0.04 us -> 9.19 us
    dot_general x24, matrix products: 58 us -> 64 us  [mult(): jnp.dot(left, right, preferred_element_type=jnp.float32, precision=lax.Pr...]
where the time goes in v1:
time: 485 us; the launch traced here: 484 us
  waiting for transfers between devices  362 us (75%)
  matrix products  64 us (13%)
  local copies, waits for them, and re-layouts  22.1 us (5%)
  other arithmetic  22 us (5%)
  between operations  13.1 us (3%)
    all_gather x4, waiting for transfers between devices, from_root(): return jnp.sum(lax.all_gather(block, axis), axis=0)  266 us
    all_gather x1, waiting for transfers between devices, body(): gathered = lax.all_gather(factor, 'rhs', axis=2, tiled=True)  95.1 us
    dot_general x24, matrix products, mult(): jnp.dot(left, right, preferred_element_type=jnp.float32, precision=lax.Pr...  64 us
    reduce_sum x4, other arithmetic, from_root(): return jnp.sum(lax.all_gather(block, axis), axis=0)  14.8 us
    dynamic_slice x4, local copies, waits for them, and re-layouts, fetch(): return lax.dynamic_slice_in_dim(gathered, first, count, 1)  12.9 us
  transfers between devices with their start and end apart: 5, of which 5 were waited for; matrix products, arithmetic and copies ran while one was open for 3% of the time, Pallas kernels for 0%

profile of v1, /device:TPU:0, one launch (start us, length us, event | category | flops | bytes accessed | tf_op | source)
XLA Modules:
  0.0 483.7 jit_solution(1685758956974951897)
XLA Ops:
  7.3 95.1 %all-gather.3.cloned.1.call-done = f32[768,12,256]{0,2,1:T(8,128)} async-done(((f32[768,12,32]{0,2,1:T(8,128)}), f32[768,12,256]{0,2,1:T(8,128)}) %all-gather.3.cloned.1.call-update) | async-done | bytes 9437200 | tf_op jit(solution)/shard_map/all_gather | solution.py:22
  102.4 374.8 %while.16 = (s32[]{:T(128)}, f32[768,512]{1,0:T(8,128)S(1)}, f32[768,512]{1,0:T(8,128)}, f32[768,12,256]{0,2,1:T(8,128)}, f32[3,256,256]{2,1,0:T(8,128)}, /*inde...) while((s32[]{:T(128)}, f32[768,512]{1,0:T(8,128)S(1)}, ...), condition=%wide.region_2.3_spmd.clone, body=%wide.region_0.2_spmd.clone.sunk | while | flops 7251820544 | bytes 81789304 | solution.py:46
  102.4 1.6 fusion.39
  104.0 2.6 convolution_subtract_fusion.4
  106.6 1.2 copy-done.1
  107.7 1.6 fusion.40
  109.3 2.6 fusion.41
  111.9 1.8 convolution_bitcast_fusion.2
  113.7 1.3 maximum_select_fusion.2
  115.0 3.2 constant_dynamic-slice_fusion.2
  118.2 65.4 %all-gather.5.cloned.1.call-done = f32[4,768,512]{2,1,0:T(8,128)} async-done(((f32[1,768,512]{2,1,0:T(8,128)}), f32[4,768,512]{2,1,0:T(8,128)}) %all-gather.5.cloned.1.call-update) | async-done | bytes 6291472 | tf_op jit(solution)/shard_map/while/body/eval_jaxpr/all_gather | solution.py:9
  183.6 3.7 reduce_sum.15
  187.3 5.9 %convolution_subtract_fusion.5 = f32[768,512]{1,0:T(8,128)S(1)} fusion(f32[768,512]{1,0:T(8,128)S(1)} %get-tuple-element.199, f32[768,768]{0,1:T(8,128)} %bitcast.54, f32[768,512]{1,0:T(8,128)S(1)} %reduce_sum.15), kind=kOutput, calls=%fused_computation.3.clone.1 | convolution fusion | flops 3624271872 | bytes 7077888 | tf_op jit(solution)/shard_map/while/body/eval_jaxpr/dot_general | solution.py:13
  193.8 1.1 copy-done.3
  194.9 1.6 fusion.39
  196.5 2.6 convolution_subtract_fusion.4
  199.1 1.2 copy-done.1
  200.2 1.6 fusion.40
  201.8 2.6 fusion.41
  204.4 1.8 convolution_bitcast_fusion.2
  206.2 1.3 maximum_select_fusion.2
  207.5 3.2 constant_dynamic-slice_fusion.2
  210.7 67.0 %all-gather.5.cloned.1.call-done = f32[4,768,512]{2,1,0:T(8,128)} async-done(((f32[1,768,512]{2,1,0:T(8,128)}), f32[4,768,512]{2,1,0:T(8,128)}) %all-gather.5.cloned.1.call-update) | async-done | bytes 6291472 | tf_op jit(solution)/shard_map/while/body/eval_jaxpr/all_gather | solution.py:9
  277.7 3.7 reduce_sum.15
  281.4 5.9 %convolution_subtract_fusion.5 = f32[768,512]{1,0:T(8,128)S(1)} fusion(f32[768,512]{1,0:T(8,128)S(1)} %get-tuple-element.199, f32[768,768]{0,1:T(8,128)} %bitcast.54, f32[768,512]{1,0:T(8,128)S(1)} %reduce_sum.15), kind=kOutput, calls=%fused_computation.3.clone.1 | convolution fusion | flops 3624271872 | bytes 7077888 | tf_op jit(solution)/shard_map/while/body/eval_jaxpr/dot_general | solution.py:13
  287.9 1.1 copy-done.3
  289.0 1.6 fusion.39
  290.6 2.6 convolution_subtract_fusion.4
  293.2 1.2 copy-done.1
  294.3 1.6 fusion.40
  295.9 2.6 fusion.41
  298.5 1.8 convolution_bitcast_fusion.2
  300.3 1.3 maximum_select_fusion.2
  301.6 3.2 constant_dynamic-slice_fusion.2
  304.8 67.0 %all-gather.5.cloned.1.call-done = f32[4,768,512]{2,1,0:T(8,128)} async-done(((f32[1,768,512]{2,1,0:T(8,128)}), f32[4,768,512]{2,1,0:T(8,128)}) %all-gather.5.cloned.1.call-update) | async-done | bytes 6291472 | tf_op jit(solution)/shard_map/while/body/eval_jaxpr/all_gather | solution.py:9
  371.8 3.7 reduce_sum.15
  375.5 5.9 %convolution_subtract_fusion.5 = f32[768,512]{1,0:T(8,128)S(1)} fusion(f32[768,512]{1,0:T(8,128)S(1)} %get-tuple-element.199, f32[768,768]{0,1:T(8,128)} %bitcast.54, f32[768,512]{1,0:T(8,128)S(1)} %reduce_sum.15), kind=kOutput, calls=%fused_computation.3.clone.1 | convolution fusion | flops 3624271872 | bytes 7077888 | tf_op jit(solution)/shard_map/while/body/eval_jaxpr/dot_general | solution.py:13
  383.1 1.6 fusion.39
  384.7 2.6 convolution_subtract_fusion.4
  387.3 1.2 copy-done.1
  388.4 1.6 fusion.40
  390.0 2.6 fusion.41
  392.6 1.8 convolution_bitcast_fusion.2
  394.4 1.3 maximum_select_fusion.2
  395.7 3.2 constant_dynamic-slice_fusion.2
  398.9 67.0 %all-gather.5.cloned.1.call-done = f32[4,768,512]{2,1,0:T(8,128)} async-done(((f32[1,768,512]{2,1,0:T(8,128)}), f32[4,768,512]{2,1,0:T(8,128)}) %all-gather.5.cloned.1.call-update) | async-done | bytes 6291472 | tf_op jit(solution)/shard_map/while/body/eval_jaxpr/all_gather | solution.py:9
  465.9 3.7 reduce_sum.15
  469.6 5.9 %convolution_subtract_fusion.5 = f32[768,512]{1,0:T(8,128)S(1)} fusion(f32[768,512]{1,0:T(8,128)S(1)} %get-tuple-element.199, f32[768,768]{0,1:T(8,128)} %bitcast.54, f32[768,512]{1,0:T(8,128)S(1)} %reduce_sum.15), kind=kOutput, calls=%fused_computation.3.clone.1 | convolution fusion | flops 3624271872 | bytes 7077888 | tf_op jit(solution)/shard_map/while/body/eval_jaxpr/dot_general | solution.py:13
  (35 shorter events, 5.0 us)
Async XLA Ops:
  6.5 95.9 %copy-start = (f32[768,512]{1,0:T(8,128)S(1)}, f32[768,512]{1,0:T(8,128)}, u32[]{:S(2)}) copy-start(f32[768,512]{1,0:T(8,128)} %param.7) | copy-start | bytes 4718596
  6.5 95.9 %all-gather.3.cloned.1.call-start = ((), (), s32[]{:S(2)}) async-start(), calls=%async_computation | async-start | bytes 10616832 | tf_op jit(solution)/shard_map/all_gather | solution.py:22
  102.4 81.2 %all-gather.5.cloned.1.call-start = ((), (), s32[]{:S(2)}) async-start(), calls=%async_computation.1 | async-start | bytes 7864320 | tf_op jit(solution)/shard_map/while/body/eval_jaxpr/all_gather | solution.py:9
  106.6 1.2 copy-start.1
  187.3 6.0 %copy-start.2 = (f32[768,512]{1,0:T(8,128)S(1)}, f32[768,512]{1,0:T(8,128)}, u32[]{:S(2)}) copy-start(f32[768,512]{1,0:T(8,128)} %get-tuple-element.200) | copy-start | bytes 4718596 | tf_op jit(solution)/shard_map/while
  193.8 1.1 copy-start.3
  194.9 82.8 %all-gather.5.cloned.1.call-start = ((), (), s32[]{:S(2)}) async-start(), calls=%async_computation.1 | async-start | bytes 7864320 | tf_op jit(solution)/shard_map/while/body/eval_jaxpr/all_gather | solution.py:9
  199.1 1.2 copy-start.1
  281.4 6.0 %copy-start.2 = (f32[768,512]{1,0:T(8,128)S(1)}, f32[768,512]{1,0:T(8,128)}, u32[]{:S(2)}) copy-start(f32[768,512]{1,0:T(8,128)} %get-tuple-element.200) | copy-start | bytes 4718596 | tf_op jit(solution)/shard_map/while
  287.9 1.1 copy-start.3
  289.0 82.8 %all-gather.5.cloned.1.call-start = ((), (), s32[]{:S(2)}) async-start(), calls=%async_computation.1 | async-start | bytes 7864320 | tf_op jit(solution)/shard_map/while/body/eval_jaxpr/all_gather | solution.py:9
  293.2 1.2 copy-start.1
  375.5 6.0 %copy-start.2 = (f32[768,512]{1,0:T(8,128)S(1)}, f32[768,512]{1,0:T(8,128)}, u32[]{:S(2)}) copy-start(f32[768,512]{1,0:T(8,128)} %get-tuple-element.200) | copy-start | bytes 4718596 | tf_op jit(solution)/shard_map/while
  382.0 1.1 copy-start.3
  383.1 82.8 %all-gather.5.cloned.1.call-start = ((), (), s32[]{:S(2)}) async-start(), calls=%async_computation.1 | async-start | bytes 7864320 | tf_op jit(solution)/shard_map/while/body/eval_jaxpr/all_gather | solution.py:9
  387.3 1.2 copy-start.1
  469.6 6.0 %copy-start.2 = (f32[768,512]{1,0:T(8,128)S(1)}, f32[768,512]{1,0:T(8,128)}, u32[]{:S(2)}) copy-start(f32[768,512]{1,0:T(8,128)} %get-tuple-element.200) | copy-start | bytes 4718596 | tf_op jit(solution)/shard_map/while
  476.1 1.1 copy-start.3
Sparse Core Ops, SparseCore 0:
  8.9 93.4 all-gather.2
  115.1 68.4 all-gather.4
  207.6 70.0 all-gather.4
  301.7 70.0 all-gather.4
  395.8 70.0 all-gather.4
